TPU v7x, 32 devices: a whole 2x2x4 slice. The times are simulated.
32 devices in a mesh: blk: 4 (over z), tok: 8 (over y, x, core).
Axes of the slice: x: 2, y: 2, z: 4, core: 2. Of those that a mesh axis runs over, the one named last changes fastest.
Arguments:
- inputs: float32 [2048, 16384], P('tok', 'blk'), may hold values from -6 to 6
- first_factor: float32 [16, 1024, 1024], P('blk', 'tok'), may hold values from -0.1875 to 0.1875
- second_factor: float32 [16, 1024, 1024], P('blk', 'tok'), may hold values from -0.1875 to 0.1875
- cotangent: float32 [2048, 16384], P('tok', 'blk'), may hold values from -6 to 6
Outputs:
- input_grad: float32 [2048, 16384], P('tok', 'blk')
- first_grad: float32 [16, 1024, 1024], P('blk', 'tok')
- second_grad: float32 [16, 1024, 1024], P('blk', 'tok')
All inputs are finite; a program needn't handle non-finite values.
Results may differ from a plain program's by a relative error of at most 0.00013.
Values sent between devices are 32-bit elements; how exact they have to be, the bound alone decides.
No kernel may reach another device: no remote copies, remote signals or barrier semaphores. Data moves between devices by JAX's collectives and lax.ppermute only.
A program may use at most 128 MiB of HBM per device.

v0:
```python
import math
import jax
import jax.numpy as jnp
from jax import lax
from jax.sharding import PartitionSpec as P


def body(inputs, first_factor, second_factor, cotangent):
    hp = lax.Precision.HIGHEST
    local_blocks = first_factor.shape[0]
    order = first_factor.shape[2]
    blocks = local_blocks * lax.axis_size("blk")
    group = order // blocks
    count = inputs.shape[0]
    xb = inputs.reshape(count, local_blocks, order)
    first_whole, second_whole = (
        lax.all_gather(first_factor, "tok", axis=1, tiled=True),
        lax.all_gather(second_factor, "tok", axis=1, tiled=True),
    )
    first_view = first_whole.reshape(local_blocks, order, blocks, group)
    first = jnp.einsum("tbi,bisg->stbg", xb, first_view, precision=hp).reshape(
        blocks, count, local_blocks * group
    )
    mixed = lax.all_to_all(first, "blk", split_axis=0, concat_axis=2, tiled=True)
    second = jnp.einsum("btk,bko->tbo", mixed, second_whole, precision=hp)
    normal_cdf = 0.5 * (1.0 + jax.scipy.special.erf(second / math.sqrt(2.0)))
    density = jnp.exp(-0.5 * second * second) / math.sqrt(2.0 * math.pi)
    delta_second = cotangent.reshape(count, local_blocks, order) * (normal_cdf + second * density)
    second_grad = jnp.einsum("btk,tbo->bko", mixed, delta_second, precision=hp)
    second_out = lax.psum_scatter(second_grad, "tok", scatter_dimension=1, tiled=True)
    delta_mixed = jnp.einsum("tbo,bko->btk", delta_second, second_whole, precision=hp)
    delta_first = lax.all_to_all(delta_mixed, "blk", split_axis=2, concat_axis=0, tiled=True)
    delta_view = delta_first.reshape(blocks, count, local_blocks, group)
    first_grad = jnp.einsum("tbi,stbg->bisg", xb, delta_view, precision=hp).reshape(
        local_blocks, order, order
    )
    input_grad = jnp.einsum("stbg,bisg->tbi", delta_view, first_view, precision=hp).reshape(
        count, local_blocks * order
    )
    first_out = lax.psum_scatter(first_grad, "tok", scatter_dimension=1, tiled=True)
    return (input_grad, first_out, second_out)


def solution(mesh):
    placed = (P("tok", "blk"), P("blk", "tok", None), P("blk", "tok", None), P("tok", "blk"))
    return jax.shard_map(
        body,
        mesh=mesh,
        in_specs=placed,
        out_specs=(P("tok", "blk"), P("blk", "tok", None), P("blk", "tok", None)),
        check_vma=False,
    )
```

profile of v0, /device:TPU:0, one launch (start us, length us, event | category | flops | bytes accessed | tf_op | source)
XLA Modules:
  0.0 574.6 jit_solution(17563923800015692502)
XLA Ops:
  7.2 0.0 all-gather.3.cloned.1.call-start
  7.2 0.7 all-gather.3.cloned.1.call-update
  7.9 0.0 all-gather.5.cloned.1.call-start
  7.9 0.7 all-gather.5.cloned.1.call-update
  8.6 6.1 %reshape.30 = f32[256,4,1024]{2,1,0:T(4,128)} reshape(f32[256,4096]{1,0:T(8,128)} %param.4) | data formatting | bytes 8388608 | tf_op jit(solution)/shard_map/reshape | solution.py:15
  14.7 87.6 %all-gather.3.cloned.1.call-done = f32[4,1024,1024]{2,1,0:T(8,128)} async-done(((f32[4,128,1024]{2,1,0:T(8,128)}), f32[4,1024,1024]{2,1,0:T(8,128)}) %all-gather.3.cloned.1.call-update) | async-done | bytes 16777232 | tf_op jit(solution)/shard_map/all_gather | solution.py:17
  102.4 16.8 %copy.43 = f32[4,1024,1024]{1,2,0:T(8,128)} copy(f32[4,1024,1024]{2,1,0:T(8,128)} %all-gather.3.cloned.1.call-done) | data formatting | bytes 33554432 | tf_op jit(solution)/shard_map/all_gather | solution.py:17
  119.1 20.6 %fusion.15 = f32[16,256,4,64]{1,3,0,2:T(8,128)S(1)} fusion(f32[4,1024,16,64]{1,3,2,0:T(8,128)} %bitcast.41, f32[256,4,1024,1]{2,1,0,3:T(4,128)} %bitcast.44), kind=kOutput, calls=%fused_computation.17 | convolution fusion | flops 12884901888 | bytes 25165824 | tf_op jit(solution)/shard_map/tbi,bisg->stbg/dot_general | solution.py:21
  139.7 2.4 copy.45
  142.2 5.2 all-to-all-start
  147.4 0.5 reduce-scatter.5.cloned.1.call-start
  147.9 5.6 copy.42
  153.5 5.4 copy.48
  158.9 82.3 %all-to-all-done = f32[16,256,256]{1,2,0:T(8,128)} async-done(((f32[16,256,256]{1,2,0:T(8,128)}), f32[16,256,256]{1,2,0:T(8,128)}, u32[]{:S(2)}, u32[]{:S(2)}) %all-to-all-start) | async-done | bytes 4194336 | tf_op jit(solution)/shard_map/all_to_all | solution.py:24
  241.2 5.2 copy.47
  246.4 5.8 %all_to_all.27 = f32[4,256,1024]{2,1,0:T(8,128)} reshape(f32[4,256,4,256]{3,2,1,0:T(4,128)} %copy.47) | data formatting | bytes 8388608 | tf_op jit(solution)/shard_map/all_to_all | solution.py:24
  252.2 21.3 %fusion.6 = f32[256,4,1024]{2,0,1:T(8,128)S(1)} fusion(f32[256,4,1024]{2,0,1:T(8,128)} %copy.48, f32[4,256,1024]{2,1,0:T(8,128)} %all_to_all.27, f32[4,1024,1024]{2,1,0:T(8,128)} %all-gather.5.cloned.1.call-done), kind=kOutput, calls=%fused_computation.7 | convolution fusion | flops 12894339072 | bytes 29360128 | tf_op jit(solution)/shard_map/btk,bko->tbo/dot_general | solution.py:25
  273.5 2.0 copy-done
  275.5 16.5 %fusion.22 = f32[4,1024,1024]{2,1,0:T(8,128)} fusion(f32[4,256,1024]{2,1,0:T(8,128)S(1)} %copy-done.1, f32[256,4,1024]{2,0,1:T(8,128)S(1)} %fusion.6), kind=kOutput, calls=%fused_computation.20 | convolution fusion | flops 12884901888 | bytes 25165824 | tf_op jit(solution)/shard_map/btk,tbo->bko/dot_general | solution.py:29
  292.1 0.0 reduce-scatter.3.cloned.1.call-start
  292.2 20.2 %fusion.21 = f32[4,256,1024]{2,1,0:T(8,128)} fusion(f32[256,4,1024]{2,0,1:T(8,128)} %copy-done, f32[4,1024,1024]{2,1,0:T(8,128)} %all-gather.5.cloned.1.call-done), kind=kOutput, calls=%fused_computation.19 | convolution fusion | flops 12884901888 | bytes 25165824 | tf_op jit(solution)/shard_map/tbo,bko->btk/dot_general | solution.py:31
  312.3 5.7 copy.49
  318.0 96.6 %all_to_all.33 = f32[4,256,1024]{1,0,2:T(4,128)S(1)} all-to-all(f32[4,256,1024]{1,0,2:T(4,128)} %copy.49), channel_id=1, replica_groups=mesh['blk'=4,'tok'=8] {'blk'}, dimensions={2} | all-to-all | bytes 8388608 | tf_op jit(solution)/shard_map/all_to_all | solution.py:32
  414.6 0.8 copy.50
  415.4 0.4 copy.51
  415.8 3.3 copy-done.2
  419.1 17.7 %fusion.10 = f32[4,16,64,1024]{3,2,1,0:T(8,128)} fusion(f32[16,256,4,64]{1,3,2,0:T(8,128)S(1)} %bitcast.50, f32[256,4,1024,1]{2,1,0,3:T(4,128)S(1)} %bitcast.45), kind=kOutput, calls=%fused_computation.12 | convolution fusion | flops 12884901888 | bytes 25165824 | tf_op jit(solution)/shard_map/tbi,stbg->bisg/dot_general | solution.py:34
  436.8 16.4 %copy.56 = f32[4,1024,1024]{2,1,0:T(8,128)} copy(f32[4,1024,1024]{1,2,0:T(8,128)} %bitcast.43) | data formatting | bytes 33554432 | tf_op jit(solution)/shard_map/reshape | solution.py:34
  453.3 20.1 %fusion.18 = f32[256,4,1024]{2,0,1:T(8,128)} fusion(f32[16,256,4,64]{1,3,2,0:T(8,128)} %bitcast.51, f32[4,1024,16,64]{1,3,2,0:T(8,128)} %bitcast.42), kind=kOutput, calls=%fused_computation.18 | convolution fusion | flops 12884901888 | bytes 25165824 | tf_op jit(solution)/shard_map/stbg,bisg->tbi/dot_general | solution.py:37
  473.3 6.0 %copy.53 = f32[256,4,1024]{0,2,1:T(8,128)} copy(f32[256,4,1024]{2,0,1:T(8,128)} %fusion.18) | data formatting | bytes 8388608 | tf_op jit(solution)/shard_map/stbg,bisg->tbi/transpose | solution.py:37
  479.3 5.7 copy.58
  485.0 82.9 %reduce-scatter.3.cloned.1.call-done = f32[4,128,1024]{2,1,0:T(8,128)} async-done(((f32[4,1024,1024]{2,1,0:T(8,128)}), f32[4,128,1024]{2,1,0:T(8,128)}) %reduce-scatter.3.cloned.1.call-update) | async-done | bytes 2097168 | tf_op jit(solution)/shard_map/reduce_scatter | solution.py:40
  (10 shorter events, 0.1 us)
Async XLA Ops:
  7.2 95.2 %all-gather.3.cloned.1.call-start = ((), (), s32[]{:S(2)}) async-start(), calls=%async_computation.4 | async-start | bytes 18874368 | tf_op jit(solution)/shard_map/all_gather | solution.py:17
  7.9 244.3 %all-gather.5.cloned.1.call-start = ((), (), s32[]{:S(2)}) async-start(), calls=%async_computation.5 | async-start | bytes 18874368 | tf_op jit(solution)/shard_map/all_gather | solution.py:18
  142.2 99.0 %all-to-all-start = ((f32[16,256,256]{1,2,0:T(8,128)}), f32[16,256,256]{1,2,0:T(8,128)}, u32[]{:S(2)}, u32[]{:S(2)}) async-start(f32[16,256,256]{1,2,0:T(8,128)} %bitcast.46), calls=%async_computation | async-start | bytes 8388608 | tf_op jit(solution)/shard_map/all_to_all | solution.py:24
  147.4 337.6 %reduce-scatter.5.cloned.1.call-start = ((), (), s32[]{:S(2)}) async-start(), calls=%async_computation.7 | async-start | bytes 18874368 | tf_op jit(solution)/shard_map/reduce_scatter | solution.py:30
  252.2 23.3 %copy-start.1 = (f32[4,256,1024]{2,1,0:T(8,128)S(1)}, f32[4,256,1024]{2,1,0:T(8,128)}, u32[]{:S(2)}) copy-start(f32[4,256,1024]{2,1,0:T(8,128)} %all_to_all.27) | copy-start | bytes 12582916
  273.5 2.0 copy-start
  292.1 275.7 %reduce-scatter.3.cloned.1.call-start = ((), (), s32[]{:S(2)}) async-start(), calls=%async_computation.6 | async-start | bytes 18874368 | tf_op jit(solution)/shard_map/reduce_scatter | solution.py:40
  415.4 3.7 copy-start.2
  415.8 21.0 %copy-start.3 = (f32[4,4,256,256]{2,3,1,0:T(8,128)}, f32[4,4,256,256]{2,3,1,0:T(8,128)S(1)}, u32[]{:S(2)}) copy-start(f32[4,4,256,256]{2,3,1,0:T(8,128)S(1)} %copy.51) | copy-start | bytes 12582916
Sparse Core Ops, SparseCore 0:
  9.9 92.4 all-gather.2
  104.3 89.7 all-gather.4
  292.2 114.3 reduce-scatter.4
  453.4 114.4 reduce-scatter.2
where the time goes:
time: 581 us; the launch traced here: 575 us
  waiting for transfers between devices  254 us (44%)
  matrix products  116 us (20%)
  blocking collectives  96.6 us (17%)
  local copies, waits for them, and re-layouts  87.6 us (15%)
  between operations  14.1 us (2%)
    all_to_all x1, blocking collectives, body(): lax.all_to_all(delta_mixed, 'blk', split_axis=2, concat_axis=0, tiled=True)  96.6 us
    all_gather x1, waiting for transfers between devices, body(): lax.all_gather(first_factor, 'tok', axis=1, tiled=True)  87.6 us
    reduce_scatter x1, waiting for transfers between devices, body(): lax.psum_scatter(first_grad, 'tok', scatter_dimension=1, tiled=True)  82.9 us
    all_to_all x1, waiting for transfers between devices, body(): lax.all_to_all(first, 'blk', split_axis=0, concat_axis=2, tiled=True)  82.3 us
    dot_general x1, matrix products, body(): second = jnp.einsum('btk,bko->tbo', mixed, second_whole, precision=hp)  21.3 us
    dot_general x1, matrix products, body(): jnp.einsum('tbi,bisg->stbg', xb, first_view, precision=hp)  20.6 us
    dot_general x1, matrix products, body(): jnp.einsum('tbo,bko->btk', delta_second, second_whole, precision=hp)  20.2 us
    dot_general x1, matrix products, body(): jnp.einsum('stbg,bisg->tbi', delta_view, first_view, precision=hp)  20.1 us
  transfers between devices with their start and end apart: 5, of which 3 were waited for; matrix products, arithmetic and copies ran while one was open for 27% of the time, Pallas kernels for 0%

commit v1 on v0

--- a/solution.py
+++ b/solution.py
@@ -14,7 +14,9 @@
     count = inputs.shape[0]
     xb = inputs.reshape(count, local_blocks, order)
     first_whole, second_whole = (
-        lax.all_gather(first_factor, "tok", axis=1, tiled=True),
+        jnp.concatenate(
+            lax.all_to_all(jnp.stack([first_factor] * lax.axis_size("tok")), "tok", 0, 0), axis=1
+        ),
         lax.all_gather(second_factor, "tok", axis=1, tiled=True),
     )
     first_view = first_whole.reshape(local_blocks, order, blocks, group)

time: 581 us -> 772 us (1.33)
  waiting for transfers between devices: 254 us -> 408 us
  local copies, waits for them, and re-layouts: 87.6 us -> 117 us
    all_to_all x0 -> x1, waiting for transfers between devices: none -> 243 us  [body(): lax.all_to_all(jnp.stack([first_factor] * lax.axis_size('tok')), 'tok', 0...]
    all_gather x1 -> x0, waiting for transfers between devices: 87.6 us -> none  [body(): lax.all_gather(first_factor, 'tok', axis=1, tiled=True)]
    another operation x0 -> x2, local copies, waits for them, and re-layouts: none -> 25.6 us  [the longest x1 18 us: body(): first_view = first_whole.reshape(local_blocks, order, blocks, group)]
    reshape x0 -> x1, local copies, waits for them, and re-layouts: none -> 17.7 us  [body(): jnp.concatenate(lax.all_to_all(jnp.stack([first_factor] * lax.axis_size('...]
    all_gather x1 -> x0, local copies, waits for them, and re-layouts: 16.8 us -> none  [body(): lax.all_gather(first_factor, 'tok', axis=1, tiled=True)]
    unnamed x10 -> x11, local copies, waits for them, and re-layouts: 16.6 us -> 18.8 us
  transfers between devices with their start and end apart: 5 -> 5, of which waited for: 3 -> 3; matrix products, arithmetic and copies ran while one was open for 27% -> 24% of each run, Pallas kernels for 0% -> 0%
where the time goes in v1:
time: 772 us; the launch traced here: 762 us
  waiting for transfers between devices  408 us (53%)
  local copies, waits for them, and re-layouts  117 us (15%)
  matrix products  116 us (15%)
  blocking collectives  96.8 us (13%)
  between operations  14.1 us (2%)
  starting transfers between devices  11.6 us (2%)
    all_to_all x1, waiting for transfers between devices, body(): lax.all_to_all(jnp.stack([first_factor] * lax.axis_size('tok')), 'tok', 0...  243 us
    all_to_all x1, blocking collectives, body(): lax.all_to_all(delta_mixed, 'blk', split_axis=2, concat_axis=0, tiled=True)  96.8 us
    reduce_scatter x1, waiting for transfers between devices, body(): lax.psum_scatter(first_grad, 'tok', scatter_dimension=1, tiled=True)  85.2 us
    all_to_all x1, waiting for transfers between devices, body(): lax.all_to_all(first, 'blk', split_axis=0, concat_axis=2, tiled=True)  79.1 us
    dot_general x1, matrix products, body(): second = jnp.einsum('btk,bko->tbo', mixed, second_whole, precision=hp)  21.2 us
    dot_general x1, matrix products, body(): jnp.einsum('tbi,bisg->stbg', xb, first_view, precision=hp)  20.6 us
    dot_general x1, matrix products, body(): jnp.einsum('stbg,bisg->tbi', delta_view, first_view, precision=hp)  19.8 us
    dot_general x1, matrix products, body(): jnp.einsum('tbo,bko->btk', delta_second, second_whole, precision=hp)  19.8 us
  transfers between devices with their start and end apart: 5, of which 3 were waited for; matrix products, arithmetic and copies ran while one was open for 24% of the time, Pallas kernels for 0%

profile of v1, /device:TPU:0, one launch (start us, length us, event | category | flops | bytes accessed | tf_op | source)
XLA Modules:
  0.0 762.4 jit_solution(14009154621496126066)
XLA Ops:
  7.2 0.7 all-gather.2.cloned.1.call-update
  7.9 1.9 copy.44
  9.8 7.6 stack.2
  17.4 6.1 all-to-all-start
  23.6 6.3 reshape.32
  29.9 242.7 %all-to-all-done = f32[8,4,128,1024]{2,3,1,0:T(8,128)} async-done(((f32[8,4,128,1024]{2,3,1,0:T(8,128)}), f32[8,4,128,1024]{2,3,1,0:T(8,128)}, u32[]{:S(2)}, u32[]{:S(2)}) %all-to-all-start) | async-done | bytes 16777248 | tf_op jit(solution)/shard_map/all_to_all | solution.py:18
  272.6 17.7 %copy.45 = f32[4,8,128,1024]{2,1,3,0:T(8,128)} copy(f32[4,8,128,1024]{2,3,0,1:T(8,128)} %bitcast.1) | data formatting | bytes 33554432 | tf_op jit(solution)/shard_map/reshape | solution.py:17
  290.2 18.0 %reshape_reshape.3 = f32[4,1024,16,64]{1,3,2,0:T(8,128)} reshape(f32[4,8,128,1024]{2,1,3,0:T(8,128)} %copy.45) | data formatting | bytes 33554432 | tf_op jit(solution)/shard_map/reshape;reshape | solution.py:22
  308.2 20.6 %fusion.15 = f32[16,256,4,64]{1,3,0,2:T(8,128)S(1)} fusion(f32[4,1024,16,64]{1,3,2,0:T(8,128)} %reshape_reshape.3, f32[256,4,1024,1]{2,1,0,3:T(4,128)} %bitcast.46), kind=kOutput, calls=%fused_computation.17 | convolution fusion | flops 12884901888 | bytes 25165824 | tf_op jit(solution)/shard_map/tbi,bisg->stbg/dot_general | solution.py:23
  328.8 2.4 copy.47
  331.3 4.8 all-to-all-start.1
  336.1 0.5 reduce-scatter.5.cloned.1.call-start
  336.6 5.6 copy.43
  342.2 5.4 copy.50
  347.7 79.1 %all-to-all-done.1 = f32[16,256,256]{1,2,0:T(8,128)} async-done(((f32[16,256,256]{1,2,0:T(8,128)}), f32[16,256,256]{1,2,0:T(8,128)}, u32[]{:S(2)}, u32[]{:S(2)}) %all-to-all-start.1) | async-done | bytes 4194336 | tf_op jit(solution)/shard_map/all_to_all | solution.py:26
  426.8 5.2 copy.49
  432.0 5.8 all_to_all.31
  437.8 21.2 %fusion.6 = f32[256,4,1024]{2,0,1:T(8,128)S(1)} fusion(f32[256,4,1024]{2,0,1:T(8,128)} %copy.50, f32[4,256,1024]{2,1,0:T(8,128)} %all_to_all.31, f32[4,1024,1024]{2,1,0:T(8,128)} %all-gather.2.cloned.1.call-done), kind=kOutput, calls=%fused_computation.7 | convolution fusion | flops 12894339072 | bytes 29360128 | tf_op jit(solution)/shard_map/btk,bko->tbo/dot_general | solution.py:27
  459.0 2.0 copy-done
  461.1 16.6 %fusion.22 = f32[4,1024,1024]{2,1,0:T(8,128)} fusion(f32[4,256,1024]{2,1,0:T(8,128)S(1)} %copy-done.1, f32[256,4,1024]{2,0,1:T(8,128)S(1)} %fusion.6), kind=kOutput, calls=%fused_computation.20 | convolution fusion | flops 12884901888 | bytes 25165824 | tf_op jit(solution)/shard_map/btk,tbo->bko/dot_general | solution.py:31
  477.7 19.8 %fusion.21 = f32[4,256,1024]{2,1,0:T(8,128)} fusion(f32[256,4,1024]{2,0,1:T(8,128)} %copy-done, f32[4,1024,1024]{2,1,0:T(8,128)} %all-gather.2.cloned.1.call-done), kind=kOutput, calls=%fused_computation.19 | convolution fusion | flops 12884901888 | bytes 25165824 | tf_op jit(solution)/shard_map/tbo,bko->btk/dot_general | solution.py:33
  497.5 5.8 copy.51
  503.2 96.8 %all_to_all.38 = f32[4,256,1024]{1,0,2:T(4,128)S(1)} all-to-all(f32[4,256,1024]{1,0,2:T(4,128)} %copy.51), channel_id=1, replica_groups=mesh['blk'=4,'tok'=8] {'blk'}, dimensions={2} | all-to-all | bytes 8388608 | tf_op jit(solution)/shard_map/all_to_all | solution.py:34
  600.0 0.8 copy.52
  600.9 0.4 copy.53
  601.3 3.3 copy-done.2
  604.6 17.7 %fusion.10 = f32[4,16,64,1024]{3,2,1,0:T(8,128)} fusion(f32[16,256,4,64]{1,3,2,0:T(8,128)S(1)} %bitcast.52, f32[256,4,1024,1]{2,1,0,3:T(4,128)S(1)} %bitcast.47), kind=kOutput, calls=%fused_computation.12 | convolution fusion | flops 12884901888 | bytes 25165824 | tf_op jit(solution)/shard_map/tbi,stbg->bisg/dot_general | solution.py:36
  622.3 16.4 %copy.58 = f32[4,1024,1024]{2,1,0:T(8,128)} copy(f32[4,1024,1024]{1,2,0:T(8,128)} %bitcast.45) | data formatting | bytes 33554432 | tf_op jit(solution)/shard_map/reshape | solution.py:36
  638.7 19.8 %fusion.18 = f32[256,4,1024]{2,0,1:T(8,128)} fusion(f32[16,256,4,64]{1,3,2,0:T(8,128)} %bitcast.53, f32[4,1024,16,64]{1,3,2,0:T(8,128)} %reshape_reshape.3), kind=kOutput, calls=%fused_computation.18 | convolution fusion | flops 12884901888 | bytes 25165824 | tf_op jit(solution)/shard_map/stbg,bisg->tbi/dot_general | solution.py:39
  658.5 6.0 copy.55
  664.5 5.9 copy.60
  670.4 85.2 %reduce-scatter.3.cloned.1.call-done = f32[4,128,1024]{2,1,0:T(8,128)} async-done(((f32[4,1024,1024]{2,1,0:T(8,128)}), f32[4,128,1024]{2,1,0:T(8,128)}) %reduce-scatter.3.cloned.1.call-update) | async-done | bytes 2097168 | tf_op jit(solution)/shard_map/reduce_scatter | solution.py:42
  (12 shorter events, 0.1 us)
Async XLA Ops:
  7.2 430.6 %all-gather.2.cloned.1.call-start = ((), (), s32[]{:S(2)}) async-start(), calls=%async_computation.5 | async-start | bytes 18874368 | tf_op jit(solution)/shard_map/all_gather | solution.py:20
  17.4 255.1 %all-to-all-start = ((f32[8,4,128,1024]{2,3,1,0:T(8,128)}), f32[8,4,128,1024]{2,3,1,0:T(8,128)}, u32[]{:S(2)}, u32[]{:S(2)}) async-start(f32[8,4,128,1024]{2,3,1,0:T(8,128)} %stack.2), calls=%async_computation | async-start | bytes 33554432 | tf_op jit(solution)/shard_map/all_to_all | solution.py:18
  331.3 95.5 %all-to-all-start.1 = ((f32[16,256,256]{1,2,0:T(8,128)}), f32[16,256,256]{1,2,0:T(8,128)}, u32[]{:S(2)}, u32[]{:S(2)}) async-start(f32[16,256,256]{1,2,0:T(8,128)} %bitcast.48), calls=%async_computation.1 | async-start | bytes 8388608 | tf_op jit(solution)/shard_map/all_to_all | solution.py:26
  336.1 334.3 %reduce-scatter.5.cloned.1.call-start = ((), (), s32[]{:S(2)}) async-start(), calls=%async_computation.7 | async-start | bytes 18874368 | tf_op jit(solution)/shard_map/reduce_scatter | solution.py:32
  437.8 23.3 %copy-start.1 = (f32[4,256,1024]{2,1,0:T(8,128)S(1)}, f32[4,256,1024]{2,1,0:T(8,128)}, u32[]{:S(2)}) copy-start(f32[4,256,1024]{2,1,0:T(8,128)} %all_to_all.31) | copy-start | bytes 12582916
  459.0 2.0 copy-start
  477.6 278.0 %reduce-scatter.3.cloned.1.call-start = ((), (), s32[]{:S(2)}) async-start(), calls=%async_computation.6 | async-start | bytes 18874368 | tf_op jit(solution)/shard_map/reduce_scatter | solution.py:42
  600.9 3.7 copy-start.2
  601.3 21.0 %copy-start.3 = (f32[4,4,256,256]{2,3,1,0:T(8,128)}, f32[4,4,256,256]{2,3,1,0:T(8,128)S(1)}, u32[]{:S(2)}) copy-start(f32[4,4,256,256]{2,3,1,0:T(8,128)S(1)} %copy.53) | copy-start | bytes 12582916
Sparse Core Ops, SparseCore 0:
  9.9 219.6 all-gather.1
  477.8 116.8 reduce-scatter.4
  638.8 116.7 reduce-scatter.2
